TPU v7x, 32 devices: a whole 2x2x4 slice. The times are simulated.
32 devices in a mesh: days: 4 (over y, x), space: 8 (over z, core).
Axes of the slice: x: 2, y: 2, z: 4, core: 2. Of those that a mesh axis runs over, the one named last changes fastest.
Arguments:
- fields: bfloat16 [640, 32, 1440], P('days', 'space')
- month_label: int32 [640], P('days'), may hold values from 0 to 11, as said below
- row_index: int32 [32], P('space'), may hold values from 0 to 31
- area_table: float32 [32], replicated, may hold values from 0.05 to 1
- basis: bfloat16 [64, 32, 1440], P(None, 'space'), may hold values from -6 to 6
Outputs:
- eofs: float32 [64, 32, 1440], P(None, 'space')
- pcs: float32 [640, 64], P('days')
Inputs may be any that keep to these rules, and one draw needn't show every extreme that they name: `month_label`: each day's label differs from floor(12 * day / 640) by at most one; the first day with a given value of floor(12 * day / 640) carries exactly that value; every month labels at least one day.
All inputs are finite; a program needn't handle non-finite values.
Results may differ from a plain program's by a relative error of at most 0.0003.
Values sent between devices are 32-bit elements; how exact they have to be, the bound alone decides.
A program may use at most 64 MiB of HBM per device.

v0:
```python
import jax
import jax.numpy as jnp
from jax import lax
from jax.sharding import PartitionSpec as P

ITERS = 2
HIGH = lax.Precision.HIGHEST


def solve_lower(lower, cover):
    shape = cover.shape
    solved = lax.linalg.triangular_solve(
        lower, cover.reshape(shape[0], -1), left_side=True, lower=True
    )
    return solved.reshape(shape)


def self_gram(cover):
    return jnp.einsum("klc,jlc->kj", cover, cover, precision=HIGH)


def local(fields, month_label, row_index, area_table, basis):
    months = jnp.arange(12, dtype=jnp.int32)
    onehot = (month_label[None, :] == months[:, None]).astype(jnp.bfloat16)
    sums = jnp.einsum("md,dlc->mlc", onehot, fields, preferred_element_type=jnp.float32)
    counts = jnp.sum(onehot.astype(jnp.float32), axis=1)
    sums, counts = lax.psum((sums, counts), "days")
    climate = sums / counts[:, None, None]
    seasonal = jnp.einsum("md,mlc->dlc", onehot.astype(jnp.float32), climate, precision=HIGH)
    table_hot = (
        row_index[:, None] == jnp.arange(area_table.shape[0], dtype=jnp.int32)[None, :]
    ).astype(jnp.float32)
    scale = jnp.sqrt(jnp.dot(table_hot, area_table, precision=HIGH))
    weighted = (fields.astype(jnp.float32) - seasonal) * scale[None, :, None]
    days_total = fields.shape[0] * lax.axis_size("days")
    partial_pcs = jnp.einsum("dlc,klc->dk", weighted, basis.astype(jnp.float32), precision=HIGH)
    pcs = lax.psum(partial_pcs, "space")
    eofs = basis.astype(jnp.float32)
    for step_count in range(ITERS):
        partial_cover = jnp.einsum("dk,dlc->klc", pcs, weighted, precision=HIGH) / days_total
        cover = lax.psum(partial_cover, "days")
        partial_gram = self_gram(cover)
        partial_raw = jnp.einsum("dlc,klc->dk", weighted, cover, precision=HIGH)
        gram, raw_pcs = lax.psum((partial_gram, partial_raw), "space")
        lower = jnp.linalg.cholesky(gram)
        eofs = solve_lower(lower, cover)
        pcs = lax.linalg.triangular_solve(
            lower, raw_pcs, left_side=False, lower=True, transpose_a=True
        )
    return (eofs, pcs)


def solution(mesh):
    placed = (P("days", "space", None), P("days"), P("space"), P(), P(None, "space", None))
    return jax.shard_map(
        local,
        mesh=mesh,
        in_specs=placed,
        out_specs=(P(None, "space", None), P("days", None)),
        check_vma=False,
    )
```

profile of v0, /device:TPU:0, one launch (start us, length us, event | category | flops | bytes accessed | tf_op | source)
XLA Modules:
  0.0 343.0 jit_solution(18154794807191105921)
XLA Ops:
  7.2 0.0 copy-start
  7.2 0.0 copy-start.5
  7.2 0.0 copy-start.4
  7.2 0.0 copy-start.7
  7.2 0.0 copy-start.6
  7.2 0.0 all-reduce.6.cloned.1.call-start
  7.3 3.1 fusion
  10.4 0.0 all-reduce.6.cloned.1.call-update
  10.4 0.0 all-reduce.8.cloned.1.call-start
  10.4 0.0 copy-done.5
  10.4 0.1 convert_reduce_fusion
  10.6 11.5 %psum.64 = f32[12]{0:T(128)S(1)} all-reduce(f32[12]{0:T(128)S(1)} %convert_reduce_fusion), channel_id=1, replica_groups=mesh['days'=4,'space'=8] {'days'}, use_global_device_ids=true, to_apply=%region_2.0 | all-reduce | flops 12 | bytes 96 | tf_op jit(solution)/shard_map/psum | solution.py:27
  22.0 0.0 copy-done.7
  22.0 0.0 copy-done.6
  22.1 0.2 fusion.4
  22.2 36.2 %all-reduce.6.cloned.1.call-done = f32[12,4,1440]{2,0,1:T(8,128)} async-done(((f32[12,4,1440]{2,0,1:T(8,128)}), f32[12,4,1440]{2,0,1:T(8,128)}) %all-reduce.6.cloned.1.call-update) | async-done | bytes 276496 | tf_op jit(solution)/shard_map/psum | solution.py:27
  58.4 0.0 copy-done.4
  58.4 3.2 subtract_multiply_fusion
  61.6 0.0 copy-start.1
  61.6 1.9 copy-done.1
  63.5 0.0 copy-done
  63.5 2.4 convolution_bitcast_fusion.4
  65.9 28.5 %psum.65 = f32[160,64]{0,1:T(8,128)S(1)} all-reduce(f32[160,64]{0,1:T(8,128)S(1)} %convolution_bitcast_fusion.4), channel_id=1, replica_groups=mesh['days'=4,'space'=8] {'space'}, use_global_device_ids=true, to_apply=%region_3.0 | all-reduce | flops 10240 | bytes 81920 | tf_op jit(solution)/shard_map/psum | solution.py:37
  94.4 5.4 %convolution_multiply_fusion.1 = f32[64,4,1440]{2,0,1:T(8,128)} fusion(f32[160,4,1440]{2,0,1:T(8,128)} %copy-done.1, f32[160,64]{0,1:T(8,128)S(1)} %psum.65), kind=kOutput, calls=%fused_computation.2 | convolution fusion | flops 708157440 | bytes 5201920 | tf_op jit(solution)/shard_map/dk,dlc->klc/dot_general | solution.py:40
  99.8 0.0 all-reduce.8.cloned.1.call-update
  99.8 0.2 all-reduce.10.cloned.1.call-start
  100.1 57.9 %all-reduce.8.cloned.1.call-done = f32[64,4,1440]{2,0,1:T(8,128)} async-done(((f32[64,4,1440]{2,0,1:T(8,128)}), f32[64,4,1440]{2,0,1:T(8,128)}) %all-reduce.8.cloned.1.call-update) | async-done | bytes 1474576 | tf_op jit(solution)/shard_map/psum | solution.py:41
  157.9 0.0 copy-start.3
  157.9 3.5 %convolution_bitcast_fusion.6 = f32[64,64]{0,1:T(8,128)S(1)} fusion(f32[64,4,1440]{2,0,1:T(8,128)} %all-reduce.8.cloned.1.call-done), kind=kOutput, calls=%fused_computation.13 | convolution fusion | flops 283115520 | bytes 1490944 | tf_op jit(solution)/shard_map/klc,jlc->kj/dot_general | solution.py:19
  161.4 0.0 copy-done.3
  161.4 5.3 %convolution_bitcast_fusion.1 = f32[160,64]{1,0:T(8,128)S(1)} fusion(f32[160,4,1440]{2,0,1:T(8,128)} %copy-done.1, f32[64,4,1440]{2,0,1:T(8,128)S(1)} %copy-done.3), kind=kOutput, calls=%fused_computation.8 | convolution fusion | flops 707788800 | bytes 5201920 | tf_op jit(solution)/shard_map/dlc,klc->dk/dot_general | solution.py:43
  166.7 29.8 %all-reduce.1 = (f32[160,64]{1,0:T(8,128)S(1)}, f32[64,64]{0,1:T(8,128)S(1)}) all-reduce(f32[160,64]{1,0:T(8,128)S(1)} %convolution_bitcast_fusion.1, f32[64,64]{0,1:T(8,128)S(1)} %convolution_bitcast_fusion.6), channel_id=1, replica_groups=mesh['days'=4,'space'=8] {'space'}, use_global_device_ids=true, to_apply=%region_8.0 | all-reduce | flops 14336 | bytes 114688 | tf_op jit(solution)/shard_map/psum | solution.py:44
  196.6 0.1 copy.16
  196.7 5.8 %cholesky.44 = f32[64,64]{1,0:T(8,128)S(1)} custom-call(f32[64,64]{1,0:T(8,128)S(1)} %fusion.15), custom_call_target="Cholesky" | custom-call | tf_op jit(solution)/shard_map/jit(cholesky)/cholesky | solution.py:45
  202.5 0.6 compare_reduce_fusion.1
  203.2 0.7 fusion.9
  203.8 4.9 %custom-call.10 = f32[1,64,64]{1,2,0:T(8,128)S(1)} custom-call(f32[1,64,64]{2,1,0:T(8,128)S(1)} %fusion.9), custom_call_target="InvertDiagBlocksLowerTriangular" | custom-call | tf_op jit(solution)/shard_map/triangular_solve/custom-call.0 | solution.py:47
  208.8 0.3 convolution_bitcast_fusion.3
  209.1 5.4 %convolution_multiply_fusion = f32[64,4,1440]{2,0,1:T(8,128)} fusion(f32[160,64,1]{0,1,2:T(8,128)S(1)} %convolution_bitcast_fusion.3, f32[160,4,1440]{2,0,1:T(8,128)} %copy-done.1), kind=kOutput, calls=%fused_computation.1 | convolution fusion | flops 708157440 | bytes 5201920 | tf_op jit(solution)/shard_map/dk,dlc->klc/dot_general | solution.py:40
  214.5 0.0 all-reduce.10.cloned.1.call-update
  214.5 58.1 %all-reduce.10.cloned.1.call-done = f32[64,4,1440]{2,0,1:T(8,128)} async-done(((f32[64,4,1440]{2,0,1:T(8,128)}), f32[64,4,1440]{2,0,1:T(8,128)}) %all-reduce.10.cloned.1.call-update) | async-done | bytes 1474576 | tf_op jit(solution)/shard_map/psum | solution.py:41
  272.6 3.6 %copy.19 = f32[64,4,1440]{2,1,0:T(4,128)} copy(f32[64,4,1440]{2,0,1:T(8,128)} %all-reduce.10.cloned.1.call-done) | data formatting | bytes 2949120 | tf_op jit(solution)/shard_map/psum | solution.py:41
  276.2 0.0 copy-start.2
  276.2 3.3 reshape.27
  279.5 0.0 copy-done.2
  279.5 5.3 %convolution_bitcast_fusion = f32[160,64]{1,0:T(8,128)S(1)} fusion(f32[160,4,1440]{2,0,1:T(8,128)} %copy-done.1, f32[64,4,1440]{2,0,1:T(8,128)S(1)} %copy-done.2), kind=kOutput, calls=%fused_computation.7 | convolution fusion | flops 707788800 | bytes 5201920 | tf_op jit(solution)/shard_map/dlc,klc->dk/dot_general | solution.py:43
  284.8 1.4 convolution_bitcast_fusion.5
  286.2 30.2 %all-reduce = (f32[64,64]{0,1:T(8,128)S(1)}, f32[160,64]{1,0:T(8,128)S(1)}) all-reduce(f32[64,64]{0,1:T(8,128)S(1)} %convolution_bitcast_fusion.5, f32[160,64]{1,0:T(8,128)S(1)} %convolution_bitcast_fusion), channel_id=1, replica_groups=mesh['days'=4,'space'=8] {'space'}, use_global_device_ids=true, to_apply=%region_10.13 | all-reduce | flops 14336 | bytes 114688 | tf_op jit(solution)/shard_map/psum | solution.py:44
  316.5 0.1 copy.18
  316.5 5.8 %cholesky.55 = f32[64,64]{1,0:T(8,128)S(1)} custom-call(f32[64,64]{1,0:T(8,128)S(1)} %fusion.13), custom_call_target="Cholesky" | custom-call | tf_op jit(solution)/shard_map/jit(cholesky)/cholesky | solution.py:45
  322.4 0.6 compare_reduce_fusion
  323.1 0.7 fusion.10
  323.7 4.9 %custom-call.8 = f32[1,64,64]{1,2,0:T(8,128)S(1)} custom-call(f32[1,64,64]{2,1,0:T(8,128)S(1)} %fusion.10), custom_call_target="InvertDiagBlocksLowerTriangular" | custom-call | tf_op jit(solution)/shard_map/triangular_solve | solution.py:12
  328.6 2.9 triangular_solve.34
  331.5 0.9 convolution_bitcast_fusion.2
  332.5 1.9 fusion.2
  334.4 2.2 copy.22
  (4 shorter events, 0.1 us)
Async XLA Ops:
  7.2 56.3 %copy-start = (bf16[64,4,1440]{2,1,0:T(4,128)(2,1)S(1)}, bf16[64,4,1440]{2,1,0:T(4,128)(2,1)}, u32[]{:S(2)}) copy-start(bf16[64,4,1440]{2,1,0:T(4,128)(2,1)} %param.12) | copy-start | bytes 2211844
  7.2 3.3 copy-start.5
  7.2 51.2 %copy-start.4 = (bf16[160,4,1440]{2,1,0:T(4,128)(2,1)S(1)}, bf16[160,4,1440]{2,1,0:T(4,128)(2,1)}, u32[]{:S(2)}) copy-start(bf16[160,4,1440]{2,1,0:T(4,128)(2,1)} %param.8) | copy-start | bytes 5529604
  7.2 14.8 %copy-start.7 = (f32[32]{0:T(128)S(1)}, f32[32]{0:T(128)}, u32[]{:S(2)}) copy-start(f32[32]{0:T(128)} %param.11) | copy-start | bytes 388
  7.2 14.8 %copy-start.6 = (s32[4]{0:T(128)S(1)}, s32[4]{0:T(128)}, u32[]{:S(2)}) copy-start(s32[4]{0:T(128)} %param.10) | copy-start | bytes 52
  7.2 51.2 %all-reduce.6.cloned.1.call-start = ((), (), s32[]{:S(2)}) async-start(), calls=%async_computation | async-start | bytes 786432 | tf_op jit(solution)/shard_map/psum | solution.py:27
  10.4 147.5 %all-reduce.8.cloned.1.call-start = ((), (), s32[]{:S(2)}) async-start(), calls=%async_computation.1 | async-start | bytes 3145728 | tf_op jit(solution)/shard_map/psum | solution.py:41
  61.6 1.9 copy-start.1
  99.8 172.8 %all-reduce.10.cloned.1.call-start = ((), (), s32[]{:S(2)}) async-start(), calls=%async_computation.2 | async-start | bytes 3145728 | tf_op jit(solution)/shard_map/psum | solution.py:41
  157.9 3.5 %copy-start.3 = (f32[64,4,1440]{2,0,1:T(8,128)S(1)}, f32[64,4,1440]{2,0,1:T(8,128)}, u32[]{:S(2)}) copy-start(f32[64,4,1440]{2,0,1:T(8,128)} %all-reduce.8.cloned.1.call-done) | copy-start | bytes 4423684
  276.2 3.3 copy-start.2
Sparse Core Ops, SparseCore 0:
  11.6 46.8 all-reduce.5
  99.9 57.9 all-reduce.7
  214.6 57.9 all-reduce.9
where the time goes:
time: 343 us
  waiting for transfers between devices  152 us (44%)
  blocking collectives  100 us (29%)
  matrix products  38.3 us (11%)
  other arithmetic  24.3 us (7%)
  local copies, waits for them, and re-layouts  14 us (4%)
  between operations  13.9 us (4%)
    psum x2, waiting for transfers between devices, local(): cover = lax.psum(partial_cover, 'days')  116 us
    psum x2, blocking collectives, local(): gram, raw_pcs = lax.psum((partial_gram, partial_raw), 'space')  60 us
    psum x1, waiting for transfers between devices, local(): sums, counts = lax.psum((sums, counts), 'days')  36.2 us
    psum x1, blocking collectives, local(): pcs = lax.psum(partial_pcs, 'space')  28.5 us
    another operation x6, other arithmetic, local(): lower = jnp.linalg.cholesky(gram)  13 us
    psum x1, blocking collectives, local(): sums, counts = lax.psum((sums, counts), 'days')  11.5 us
    dot_general x2, matrix products, local(): jnp.einsum('dk,dlc->klc', pcs, weighted, precision=HIGH) / days_total  10.8 us
    dot_general x2, matrix products, local(): partial_raw = jnp.einsum('dlc,klc->dk', weighted, cover, precision=HIGH)  10.6 us
  transfers between devices with their start and end apart: 3, of which 3 were waited for; matrix products, arithmetic and copies ran while one was open for 0% of the time, Pallas kernels for 0%

commit v1 on v0

--- a/solution.py
+++ b/solution.py
@@ -1,3 +1,4 @@
+import functools
 import jax
 import jax.numpy as jnp
 from jax import lax
@@ -5,6 +6,17 @@
 
 ITERS = 2
 HIGH = lax.Precision.HIGHEST
+
+
+def case_define(page, link_axis):
+    heard = page
+    sides = lax.axis_size(link_axis)
+    for dev_i in [[(nth, nth ^ u) for nth in range(sides)] for u in (1, 2, 4, 8, 16) if u < sides]:
+        heard = heard + lax.ppermute(heard, link_axis, dev_i)
+    return heard
+
+
+expand_runs = functools.partial(case_define, link_axis="days")
 
 
 def solve_lower(lower, cover):
@@ -38,7 +50,7 @@
     eofs = basis.astype(jnp.float32)
     for step_count in range(ITERS):
         partial_cover = jnp.einsum("dk,dlc->klc", pcs, weighted, precision=HIGH) / days_total
-        cover = lax.psum(partial_cover, "days")
+        cover = expand_runs(partial_cover)
         partial_gram = self_gram(cover)
         partial_raw = jnp.einsum("dlc,klc->dk", weighted, cover, precision=HIGH)
         gram, raw_pcs = lax.psum((partial_gram, partial_raw), "space")

time: 343 us -> 354 us (1.032)
  blocking collectives: 100 us -> 109 us
  matrix products: 38.3 us -> 29.8 us
  waiting for transfers between devices: 152 us -> 160 us
  starting transfers between devices: 0.3 us -> 5.91 us
    ppermute x0 -> x4, waiting for transfers between devices: none -> 124 us  [case_define(): heard = heard + lax.ppermute(heard, link_axis, dev_i)]
    psum x2 -> x0, waiting for transfers between devices: 116 us -> none  [local(): cover = lax.psum(partial_cover, 'days')]
    psum x2, blocking collectives: 60 us -> 68.5 us  [local(): gram, raw_pcs = lax.psum((partial_gram, partial_raw), 'space')]
    ppermute x0 -> x4, starting transfers between devices: none -> 5.87 us  [case_define(): heard = heard + lax.ppermute(heard, link_axis, dev_i)]
    dot_general x2, matrix products: 10.6 us -> 6.39 us  [local(): partial_raw = jnp.einsum('dlc,klc->dk', weighted, cover, precision=HIGH)]
    psum x1 -> x0, local copies, waits for them, and re-layouts: 3.56 us -> none  [local(): cover = lax.psum(partial_cover, 'days')]
  transfers between devices with their start and end apart: 3 -> 5, of which waited for: 3 -> 5; matrix products, arithmetic and copies ran while one was open for 0% -> 0% of each run, Pallas kernels for 0% -> 0%
where the time goes in v1:
time: 354 us
  waiting for transfers between devices  160 us (45%)
  blocking collectives  109 us (31%)
  matrix products  29.8 us (8%)
  other arithmetic  25 us (7%)
  between operations  14.3 us (4%)
  local copies, waits for them, and re-layouts  10.5 us (3%)
  starting transfers between devices  5.91 us (2%)
    ppermute x4, waiting for transfers between devices, case_define(): heard = heard + lax.ppermute(heard, link_axis, dev_i)  124 us
    psum x2, blocking collectives, local(): gram, raw_pcs = lax.psum((partial_gram, partial_raw), 'space')  68.5 us
    psum x1, waiting for transfers between devices, local(): sums, counts = lax.psum((sums, counts), 'days')  36.2 us
    psum x1, blocking collectives, local(): pcs = lax.psum(partial_pcs, 'space')  28.5 us
    another operation x6, other arithmetic, local(): lower = jnp.linalg.cholesky(gram)  13 us
    psum x1, blocking collectives, local(): sums, counts = lax.psum((sums, counts), 'days')  11.5 us
    dot_general x2, matrix products, local(): jnp.einsum('dk,dlc->klc', pcs, weighted, precision=HIGH) / days_total  8.56 us
  transfers between devices with their start and end apart: 5, of which 5 were waited for; matrix products, arithmetic and copies ran while one was open for 0% of the time, Pallas kernels for 0%

profile of v1, /device:TPU:0, one launch (start us, length us, event | category | flops | bytes accessed | tf_op | source)
XLA Modules:
  0.0 353.8 jit_solution(15513263034136418239)
XLA Ops:
  7.2 0.0 copy-start
  7.2 0.0 copy-start.5
  7.2 0.0 copy-start.4
  7.2 0.0 copy-start.7
  7.2 0.0 copy-start.6
  7.2 0.0 all-reduce.4.cloned.1.call-start
  7.3 3.1 fusion
  10.4 0.0 all-reduce.4.cloned.1.call-update
  10.4 0.0 copy-done.5
  10.4 0.1 convert_reduce_fusion
  10.5 11.5 %psum.50 = f32[12]{0:T(128)S(1)} all-reduce(f32[12]{0:T(128)S(1)} %convert_reduce_fusion), channel_id=1, replica_groups=mesh['days'=4,'space'=8] {'days'}, use_global_device_ids=true, to_apply=%region_2.0 | all-reduce | flops 12 | bytes 96 | tf_op jit(solution)/shard_map/psum | solution.py:39
  22.0 0.0 copy-done.7
  22.0 0.0 copy-done.6
  22.0 0.2 fusion.4
  22.2 36.2 %all-reduce.4.cloned.1.call-done = f32[12,4,1440]{2,0,1:T(8,128)} async-done(((f32[12,4,1440]{2,0,1:T(8,128)}), f32[12,4,1440]{2,0,1:T(8,128)}) %all-reduce.4.cloned.1.call-update) | async-done | bytes 276496 | tf_op jit(solution)/shard_map/psum | solution.py:39
  58.4 0.0 copy-done.4
  58.4 3.2 subtract_multiply_fusion
  61.6 0.0 copy-start.1
  61.6 1.9 copy-done.1
  63.5 0.0 copy-done
  63.5 2.4 convolution_bitcast_fusion.4
  65.9 28.5 %psum.51 = f32[160,64]{0,1:T(8,128)S(1)} all-reduce(f32[160,64]{0,1:T(8,128)S(1)} %convolution_bitcast_fusion.4), channel_id=1, replica_groups=mesh['days'=4,'space'=8] {'space'}, use_global_device_ids=true, to_apply=%region_3.0 | all-reduce | flops 10240 | bytes 81920 | tf_op jit(solution)/shard_map/psum | solution.py:49
  94.4 4.3 %convolution_multiply_fusion.1 = f32[64,4,1440]{2,0,1:T(8,128)S(1)} fusion(f32[160,4,1440]{2,0,1:T(8,128)} %copy-done.1, f32[160,64]{0,1:T(8,128)S(1)} %psum.51), kind=kOutput, calls=%fused_computation.2 | convolution fusion | flops 708157440 | bytes 5201920 | tf_op jit(solution)/shard_map/dk,dlc->klc/dot_general | solution.py:52
  98.7 1.5 collective-permute-start
  100.2 31.3 %collective-permute-done = f32[64,4,1440]{2,0,1:T(8,128)S(1)} collective-permute-done((f32[64,4,1440]{2,0,1:T(8,128)S(1)}, f32[64,4,1440]{2,0,1:T(8,128)S(1)}, u32[]{:S(2)}, u32[]{:S(2)}) %collective-permute-start) | collective-permute-done | bytes 1474592 | tf_op jit(solution)/shard_map/ppermute | solution.py:15
  131.5 0.0 copy-start.2
  131.5 0.3 add.36
  131.8 1.4 collective-permute-start.1
  133.2 30.5 %collective-permute-done.1 = f32[64,4,1440]{2,0,1:T(8,128)S(1)} collective-permute-done((f32[64,4,1440]{2,0,1:T(8,128)S(1)}, f32[64,4,1440]{2,0,1:T(8,128)S(1)}, u32[]{:S(2)}, u32[]{:S(2)}) %collective-permute-start.1) | collective-permute-done | bytes 1474592 | tf_op jit(solution)/shard_map/ppermute | solution.py:15
  163.7 1.4 convolution_bitcast_fusion.6
  165.1 0.0 copy-done.2
  165.1 3.2 convolution_bitcast_fusion.1
  168.3 34.3 %all-reduce.1 = (f32[160,64]{1,0:T(8,128)S(1)}, f32[64,64]{0,1:T(8,128)S(1)}) all-reduce(f32[160,64]{1,0:T(8,128)S(1)} %convolution_bitcast_fusion.1, f32[64,64]{0,1:T(8,128)S(1)} %convolution_bitcast_fusion.6), channel_id=1, replica_groups=mesh['days'=4,'space'=8] {'space'}, use_global_device_ids=true, to_apply=%region_7.0 | all-reduce | flops 14336 | bytes 114688 | tf_op jit(solution)/shard_map/psum | solution.py:56
  202.7 0.1 copy.16
  202.8 5.8 %cholesky.44 = f32[64,64]{1,0:T(8,128)S(1)} custom-call(f32[64,64]{1,0:T(8,128)S(1)} %fusion.17), custom_call_target="Cholesky" | custom-call | tf_op jit(solution)/shard_map/jit(cholesky)/cholesky | solution.py:57
  208.7 0.6 compare_reduce_fusion.1
  209.3 0.7 fusion.11
  210.0 4.9 %custom-call.10 = f32[1,64,64]{1,2,0:T(8,128)S(1)} custom-call(f32[1,64,64]{2,1,0:T(8,128)S(1)} %fusion.11), custom_call_target="InvertDiagBlocksLowerTriangular" | custom-call | tf_op jit(solution)/shard_map/triangular_solve/custom-call.0 | solution.py:59
  214.9 0.3 convolution_bitcast_fusion.3
  215.2 4.3 %convolution_multiply_fusion = f32[64,4,1440]{2,0,1:T(8,128)S(1)} fusion(f32[160,64,1]{0,1,2:T(8,128)S(1)} %convolution_bitcast_fusion.3, f32[160,4,1440]{2,0,1:T(8,128)} %copy-done.1), kind=kOutput, calls=%fused_computation.1 | convolution fusion | flops 708157440 | bytes 5201920 | tf_op jit(solution)/shard_map/dk,dlc->klc/dot_general | solution.py:52
  219.5 1.5 collective-permute-start.2
  221.0 31.3 %collective-permute-done.2 = f32[64,4,1440]{2,0,1:T(8,128)S(1)} collective-permute-done((f32[64,4,1440]{2,0,1:T(8,128)S(1)}, f32[64,4,1440]{2,0,1:T(8,128)S(1)}, u32[]{:S(2)}, u32[]{:S(2)}) %collective-permute-start.2) | collective-permute-done | bytes 1474592 | tf_op jit(solution)/shard_map/ppermute | solution.py:15
  252.3 0.2 add.38
  252.5 0.0 copy-start.3
  252.5 1.4 collective-permute-start.3
  253.9 30.5 %collective-permute-done.3 = f32[64,4,1440]{2,0,1:T(8,128)S(1)} collective-permute-done((f32[64,4,1440]{2,0,1:T(8,128)S(1)}, f32[64,4,1440]{2,0,1:T(8,128)S(1)}, u32[]{:S(2)}, u32[]{:S(2)}) %collective-permute-start.3) | collective-permute-done | bytes 1474592 | tf_op jit(solution)/shard_map/ppermute | solution.py:15
  284.4 0.2 add.39
  284.7 0.0 copy-done.3
  284.7 3.2 convolution_bitcast_fusion
  287.9 1.4 convolution_bitcast_fusion.5
  289.3 1.0 copy.19
  290.3 2.4 reshape.27
  292.6 34.2 %all-reduce = (f32[64,64]{0,1:T(8,128)S(1)}, f32[160,64]{1,0:T(8,128)S(1)}) all-reduce(f32[64,64]{0,1:T(8,128)S(1)} %convolution_bitcast_fusion.5, f32[160,64]{1,0:T(8,128)S(1)} %convolution_bitcast_fusion), channel_id=1, replica_groups=mesh['days'=4,'space'=8] {'space'}, use_global_device_ids=true, to_apply=%region_8.11 | all-reduce | flops 14336 | bytes 114688 | tf_op jit(solution)/shard_map/psum | solution.py:56
  326.9 0.1 copy.18
  327.0 5.8 %cholesky.55 = f32[64,64]{1,0:T(8,128)S(1)} custom-call(f32[64,64]{1,0:T(8,128)S(1)} %fusion.15), custom_call_target="Cholesky" | custom-call | tf_op jit(solution)/shard_map/jit(cholesky)/cholesky | solution.py:57
  332.8 0.6 compare_reduce_fusion
  333.5 0.7 fusion.12
  334.1 4.9 %custom-call.8 = f32[1,64,64]{1,2,0:T(8,128)S(1)} custom-call(f32[1,64,64]{2,1,0:T(8,128)S(1)} %fusion.12), custom_call_target="InvertDiagBlocksLowerTriangular" | custom-call | tf_op jit(solution)/shard_map/triangular_solve | solution.py:24
  339.0 2.9 triangular_solve.34
  341.9 0.9 convolution_bitcast_fusion.2
  342.9 1.9 fusion.2
  344.8 2.2 copy.22
  (4 shorter events, 0.1 us)
Async XLA Ops:
  7.2 56.3 %copy-start = (bf16[64,4,1440]{2,1,0:T(4,128)(2,1)S(1)}, bf16[64,4,1440]{2,1,0:T(4,128)(2,1)}, u32[]{:S(2)}) copy-start(bf16[64,4,1440]{2,1,0:T(4,128)(2,1)} %param.12) | copy-start | bytes 2211844
  7.2 3.2 copy-start.5
  7.2 51.2 %copy-start.4 = (bf16[160,4,1440]{2,1,0:T(4,128)(2,1)S(1)}, bf16[160,4,1440]{2,1,0:T(4,128)(2,1)}, u32[]{:S(2)}) copy-start(bf16[160,4,1440]{2,1,0:T(4,128)(2,1)} %param.8) | copy-start | bytes 5529604
  7.2 14.8 %copy-start.7 = (f32[32]{0:T(128)S(1)}, f32[32]{0:T(128)}, u32[]{:S(2)}) copy-start(f32[32]{0:T(128)} %param.11) | copy-start | bytes 388
  7.2 14.8 %copy-start.6 = (s32[4]{0:T(128)S(1)}, s32[4]{0:T(128)}, u32[]{:S(2)}) copy-start(s32[4]{0:T(128)} %param.10) | copy-start | bytes 52
  7.2 51.2 %all-reduce.4.cloned.1.call-start = ((), (), s32[]{:S(2)}) async-start(), calls=%async_computation | async-start | bytes 786432 | tf_op jit(solution)/shard_map/psum | solution.py:39
  61.6 1.9 copy-start.1
  98.7 32.8 %collective-permute-start = (f32[64,4,1440]{2,0,1:T(8,128)S(1)}, f32[64,4,1440]{2,0,1:T(8,128)S(1)}, u32[]{:S(2)}, u32[]{:S(2)}) collective-permute-start(f32[64,4,1440]{2,0,1:T(8,128)S(1)} %convolution_multiply_fusion.1), channel_id=1, source_target_pairs={{0,8},{8,0},{16,24},{24,16},{1,9},{9,1},{17,25},{25,17},{2,10},{10... | collective-permute-start | bytes 4423688 | tf_op jit(solution)/shard_map/ppermute | solution.py:15
  131.5 33.6 %copy-start.2 = (f32[160,4,1440]{2,0,1:T(8,128)S(1)}, f32[160,4,1440]{2,0,1:T(8,128)}, u32[]{:S(2)}) copy-start(f32[160,4,1440]{2,0,1:T(8,128)} %copy-done.1) | copy-start | bytes 11059204
  131.8 32.0 %collective-permute-start.1 = (f32[64,4,1440]{2,0,1:T(8,128)S(1)}, f32[64,4,1440]{2,0,1:T(8,128)S(1)}, u32[]{:S(2)}, u32[]{:S(2)}) collective-permute-start(f32[64,4,1440]{2,0,1:T(8,128)S(1)} %add.36), channel_id=1, source_target_pairs={{0,16},{8,24},{16,0},{24,8},{1,17},{9,25},{17,1},{25,9},{2,18},{10... | collective-permute-start | bytes 4423688 | tf_op jit(solution)/shard_map/ppermute | solution.py:15
  219.5 32.8 %collective-permute-start.2 = (f32[64,4,1440]{2,0,1:T(8,128)S(1)}, f32[64,4,1440]{2,0,1:T(8,128)S(1)}, u32[]{:S(2)}, u32[]{:S(2)}) collective-permute-start(f32[64,4,1440]{2,0,1:T(8,128)S(1)} %convolution_multiply_fusion), channel_id=1, source_target_pairs={{0,8},{8,0},{16,24},{24,16},{1,9},{9,1},{17,25},{25,17},{2,10},{10... | collective-permute-start | bytes 4423688 | tf_op jit(solution)/shard_map/ppermute | solution.py:15
  252.5 32.2 %copy-start.3 = (f32[160,4,1440]{2,0,1:T(8,128)S(1)}, f32[160,4,1440]{2,0,1:T(8,128)}, u32[]{:S(2)}) copy-start(f32[160,4,1440]{2,0,1:T(8,128)} %copy-done.1) | copy-start | bytes 11059204
  252.5 31.9 %collective-permute-start.3 = (f32[64,4,1440]{2,0,1:T(8,128)S(1)}, f32[64,4,1440]{2,0,1:T(8,128)S(1)}, u32[]{:S(2)}, u32[]{:S(2)}) collective-permute-start(f32[64,4,1440]{2,0,1:T(8,128)S(1)} %add.38), channel_id=1, source_target_pairs={{0,16},{8,24},{16,0},{24,8},{1,17},{9,25},{17,1},{25,9},{2,18},{10... | collective-permute-start | bytes 4423688 | tf_op jit(solution)/shard_map/ppermute | solution.py:15
Sparse Core Ops, SparseCore 0:
  11.6 46.8 all-reduce.3
